TPU v7x, 32 devices: a whole 2x2x4 slice. The times are simulated.
32 devices in a mesh: grp: 2 (over y), seq: 8 (over z, x), head: 2 (over core).
Axes of the slice: x: 2, y: 2, z: 4, core: 2. Of those that a mesh axis runs over, the one named last changes fastest.
Arguments:
- query_rows: bfloat16 [16, 32, 128], P('grp', 'head'), parts along dimension 0, may hold values from -100 to 100
- cache_keys: bfloat16 [512, 8, 128, 128], P(('grp', 'seq'), 'head'), parts along dimension 0, may hold values from -5 to 5
- cache_values: bfloat16 [512, 8, 128, 128], P(('grp', 'seq'), 'head'), parts along dimension 0, may hold values from -6 to 6
- page_table: int32 [512], P('grp'), parts along dimension 0, may hold values from 0 to 255, as said below
- seq_lengths: int32 [16], P('grp'), parts along dimension 0, may hold values from 128 to 4096, as said below
Outputs:
- attended: bfloat16 [16, 32, 128], P('grp', 'head'), parts along dimension 0
There are 2 independent parts, one for each index of `grp`. A program takes and returns all parts, laid end to end along the dimension named above; each array names one. Nothing has to cross between parts.
Inputs may be any that keep to these rules, and one draw needn't show every extreme that they name: `page_table`: entry b * 32 + j is the pool slot of page j of sequence b; slot s lies on index s // 32 of seq; every slot appears once. `seq_lengths`: some sequence has exactly 4096 tokens.
All inputs are finite; a program needn't handle non-finite values.
Results may differ from a plain program's by a relative error of at most 0.0029.
Values may be sent and summed in bfloat16 or wider, within the bound.
A program may use at most 64 MiB of HBM per device.

v0:
```python
import functools
import math

import jax
import jax.numpy as jnp
from jax import lax
from jax.experimental import pallas as pl
from jax.experimental.pallas import tpu as pltpu
from jax.sharding import PartitionSpec as P

MESH = pl.DeviceIdType.MESH
VERY_LOW = -1e30
FLOOR = -1e29


def attend(
    n,
    table_width,
    q_hbm,
    k_hbm,
    v_hbm,
    pt_hbm,
    len_hbm,
    out_ref,
    q_raw,
    q_rows,
    pt_vmem,
    len_smem,
    k_vmem,
    v_vmem,
    mask_ref,
    stat_out,
    stat_in,
    num_out,
    num_in,
    small_sem,
    k_sem,
    v_sem,
    stat_send,
    stat_recv,
    num_send,
    num_recv,
    fin_send,
    fin_recv,
):
    me = lax.axis_index("seq")
    batch, heads, head_dim = q_raw.shape
    kv_heads, slots, page, _ = k_vmem.shape
    group = heads // kv_heads
    rows = group * batch
    per_dev = out_ref.shape[1]
    pool = pt_vmem.shape[0]

    small = (
        pltpu.make_async_copy(q_hbm, q_raw, small_sem.at[0]),
        pltpu.make_async_copy(pt_hbm, pt_vmem, small_sem.at[1]),
        pltpu.make_async_copy(len_hbm, len_smem, small_sem.at[2]),
    )
    for copy in small:
        copy.start()
    k_copies, v_copies = [], []
    for g in range(kv_heads):
        k_copies.append(pltpu.make_async_copy(k_hbm.at[:, g], k_vmem.at[g], k_sem.at[g]))
        v_copies.append(pltpu.make_async_copy(v_hbm.at[:, g], v_vmem.at[g], v_sem.at[g]))

    order = [(k_copies, g, 2 * g) for g in range(kv_heads)]
    order += [(v_copies, g, 2 * g + 3) for g in range(kv_heads)]
    for copies, g, _ in sorted(order, key=lambda item: item[2]):
        copies[g].start()

    barrier = pltpu.get_barrier_semaphore()
    for step in range(1, n):
        pl.semaphore_signal(
            barrier, inc=1, device_id={"seq": lax.rem(me + step, n)}, device_id_type=MESH
        )

    small[0].wait()
    stat_out[...] = jnp.zeros_like(stat_out)

    q_rows[...] = q_raw[...].astype(jnp.float32).reshape(batch * heads, head_dim)

    factor = math.log2(math.e) / math.sqrt(head_dim)
    half = lax.broadcasted_iota(jnp.int32, (rows, head_dim), 1) < head_dim // 2
    per_group = rows // per_dev

    def stat_copy(dest, slot):
        return pltpu.make_async_remote_copy(
            src_ref=stat_out.at[dest],
            dst_ref=stat_in.at[slot],
            send_sem=stat_send.at[dest],
            recv_sem=stat_recv.at[slot],
            device_id={"seq": dest},
            device_id_type=MESH,
        )

    def num_copy(dest, slot):
        return pltpu.make_async_remote_copy(
            src_ref=num_out.at[dest],
            dst_ref=num_in.at[slot],
            send_sem=num_send.at[dest],
            recv_sem=num_recv.at[slot],
            device_id={"seq": dest},
            device_id_type=MESH,
        )

    def fin_copy(dest, slot):
        return pltpu.make_async_remote_copy(
            src_ref=out_ref.at[slot],
            dst_ref=out_ref.at[slot],
            send_sem=fin_send.at[dest],
            recv_sem=fin_recv.at[slot],
            device_id={"seq": dest},
            device_id_type=MESH,
        )

    def send(make, dest):
        @pl.when(dest != me)
        def _():
            make(dest, me).start()

    def score(g):
        q_g = jnp.concatenate(
            [q_rows[pl.ds(g * group + h, batch, stride=heads), :] for h in range(group)], axis=0
        ).astype(jnp.bfloat16)
        return lax.dot_general(
            q_g,
            k_vmem[g].reshape(slots * page, head_dim),
            (((1,), (1,)), ((), ())),
            preferred_element_type=jnp.float32,
        )

    def soften(scores):
        scores = scores + jnp.concatenate([mask_ref[...]] * group, axis=0)
        top = jnp.maximum(jnp.max(scores, axis=1, keepdims=True), FLOOR)
        weights = jnp.exp2((scores - top) * factor)
        total = jnp.sum(weights, axis=1, keepdims=True)
        high = weights.astype(jnp.bfloat16)
        return jnp.where(half, top, total), high

    def gather(g, weights):
        numer = jnp.dot(
            weights,
            v_vmem[g].reshape(slots * page, head_dim),
            preferred_element_type=jnp.float32,
        )
        return numer

    def post_stats(stats):
        stats = jnp.concatenate(stats, axis=0).T
        for dest in range(n):
            for row in range(2):
                line = row * (head_dim // 2)
                stat_out[dest, row : row + 1, :per_dev] = stats[
                    line : line + 1, dest * per_dev : (dest + 1) * per_dev
                ]
            waiting.append((stat_copy, dest))

    def post_numer(g, numer):
        for i in range(per_group):
            dest = g * per_group + i
            num_out[dest] = numer[i * per_dev : (i + 1) * per_dev]
            waiting.append((num_copy, dest))

    def build_mask():
        entry = lax.broadcasted_iota(jnp.int32, (1, pool), 1)
        span = 8 * page
        code = jnp.zeros((1, pool), jnp.int32)
        for b in range(batch):
            live = jnp.clip(len_smem[b] - page * (entry - b * table_width), 0, page)
            code = jnp.where(entry >= b * table_width, b * span + live, code)
        slot_ids = me * slots + lax.broadcasted_iota(jnp.int32, (slots, pool), 0)
        hit = pt_vmem[...].reshape(1, pool) == slot_ids
        slot_code = jnp.sum(
            jnp.where(hit, code.astype(jnp.float32), 0.0), axis=1, keepdims=True
        )
        slot_code = jnp.broadcast_to(slot_code, (slots, page))
        base = (lax.broadcasted_iota(jnp.int32, (batch, page), 0) * span).astype(jnp.float32)
        token = lax.broadcasted_iota(jnp.int32, (batch, page), 1).astype(jnp.float32)
        for s in range(slots):
            left = slot_code[s : s + 1, :] - base
            live = (token < left) & (left <= float(page))
            mask_ref[:, s * page : (s + 1) * page] = jnp.where(live, 0.0, VERY_LOW)

    scores, weights, stats, waiting = {}, {}, [], []
    opening = kv_heads + -1
    for t in range(kv_heads + 2):
        if t == 0:
            small[1].wait()
            small[2].wait()
        if t < kv_heads:
            k_copies[t].wait()
        if t >= 2:
            v_copies[t - 2].wait()
        if t < kv_heads:
            scores[t] = score(t)
        if t == 0:
            build_mask()
        if 1 <= t <= kv_heads:
            tops_here, weights[t - 1] = soften(scores.pop(t - 1))
            stats.append(tops_here)
        if t >= 2:
            numer = gather(t - 2, weights.pop(t - 2))
        if t == kv_heads:
            post_stats(stats)
        if t >= 2:
            post_numer(t - 2, numer)
        if t == opening:
            pl.semaphore_wait(barrier, n - 1)
        if t >= opening:
            for make, dest in waiting:
                send(make, dest)
            waiting = []

    stat_in[me] = stat_out[me]
    num_in[me] = num_out[me]
    for step in range(1, n):
        stat_copy(0, lax.rem(me + step, n)).wait_recv()
    tops, totals = stat_in[:, 0, :], stat_in[:, 1, :]
    scales = jnp.exp2((tops - jnp.max(tops, axis=0, keepdims=True)) * factor)
    scales = (scales / jnp.sum(scales * totals, axis=0, keepdims=True)).T[:per_dev]
    scales = [jnp.broadcast_to(scales[:, s : s + 1], (per_dev, head_dim)) for s in range(n)]
    for step in range(1, n):
        num_copy(0, lax.rem(me + step, n)).wait_recv()
    result = sum(scales[s] * num_in[s] for s in range(n))
    out_ref[me] = result.astype(out_ref.dtype)
    for step in range(1, n):
        fin_copy(lax.rem(me + step, n), me).start()
    for dest in range(n):
        @pl.when(dest != me)
        def _():
            stat_copy(dest, me).wait_send()
            num_copy(dest, me).wait_send()
    for step in range(1, n):
        fin_copy(0, lax.rem(me + step, n)).wait_recv()
    for step in range(1, n):
        fin_copy(lax.rem(me + step, n), me).wait_send()


def shards(n, query_rows, cache_keys, cache_values, page_table, seq_lengths):
    slots, kv_heads, page, head_dim = cache_keys.shape
    batch, heads, _ = query_rows.shape
    pool = page_table.shape[0]
    per_dev = batch * heads // n
    f32, bf16 = jnp.float32, jnp.bfloat16
    hbm = pl.BlockSpec(memory_space=pl.ANY)
    out = pl.pallas_call(
        functools.partial(attend, n, pool // batch),
        out_shape=pltpu.VMEM((n, per_dev, head_dim), bf16),
        in_specs=[hbm] * 5,
        out_specs=pl.BlockSpec(memory_space=pltpu.VMEM),
        scratch_shapes=[
            pltpu.VMEM((batch, heads, head_dim), bf16),
            pltpu.VMEM((batch * heads, head_dim), f32),
            pltpu.VMEM((pool,), jnp.int32),
            pltpu.SMEM((batch,), jnp.int32),
            pltpu.VMEM((kv_heads, slots, page, head_dim), bf16),
            pltpu.VMEM((kv_heads, slots, page, head_dim), bf16),
            pltpu.VMEM((batch, slots * page), f32),
            pltpu.VMEM((n, 2, head_dim), f32),
            pltpu.VMEM((n, 2, head_dim), f32),
            pltpu.VMEM((n, per_dev, head_dim), f32),
            pltpu.VMEM((n, per_dev, head_dim), f32),
            pltpu.SemaphoreType.DMA((3,)),
            pltpu.SemaphoreType.DMA((kv_heads,)),
            pltpu.SemaphoreType.DMA((kv_heads,)),
        ]
        + [pltpu.SemaphoreType.DMA((n,))] * 6,
        compiler_params=pltpu.CompilerParams(collective_id=0, has_side_effects=True),
    )(query_rows, cache_keys, cache_values, page_table, seq_lengths)
    return out.reshape(heads, batch, head_dim).transpose(1, 0, 2)


def solution(mesh):
    in_specs = (
        P("grp", "head", None),
        P(("grp", "seq"), "head", None, None),
        P(("grp", "seq"), "head", None, None),
        P("grp"),
        P("grp"),
    )
    return jax.shard_map(
        functools.partial(shards, mesh.shape["seq"]),
        mesh=mesh,
        in_specs=in_specs,
        out_specs=P("grp", "head", None),
        check_vma=False,
    )
```

profile of v0, /device:TPU:0, one launch (start us, length us, event | category | flops | bytes accessed | tf_op | source)
XLA Modules:
  0.0 16.9 jit_solution(334407445290594400)
XLA Ops:
  0.0 16.2 %shard_map.55 = bf16[8,16,128]{2,1,0:T(8,128)(2,1)S(1)} custom-call(bf16[8,16,128]{2,1,0:T(8,128)(2,1)} %q_hbm.1, bf16[32,4,128,128]{3,2,1,0:T(8,128)(2,1)} %k_hbm.1, bf16[32,4,128,128]{3,2,1,0:T(8,128)(2,1)} %v_hbm.1, s32[256]{0:T(256)} %pt_hbm.1, s32[8]{0:T(128)} %len_hbm.1), custom_call_target="tpu_custom_call" | custom-call | tf_op jit(solution)/shard_map/pallas_call | solution.py:246
  16.2 0.6 %copy.8 = bf16[16,8,128]{2,0,1:T(8,128)(2,1)} copy(bf16[16,8,128]{2,1,0:T(8,128)(2,1)S(1)} %bitcast.4) | data formatting | bytes 65536 | tf_op jit(solution)/shard_map/reshape | solution.py:270
where the time goes:
time: 17 us; the launch traced here: 16.9 us
  Pallas kernels  16.2 us (95%)
  local copies, waits for them, and re-layouts  0.62 us (4%)
    pallas_call x1, Pallas kernels, shards(): pl.pallas_call(functools.partial(attend, n, pool // batch), out_shape=plt...  16.2 us
    reshape x1, local copies, waits for them, and re-layouts, shards(): return out.reshape(heads, batch, head_dim).transpose(1, 0, 2)  0.62 us

commit v1 on v0

v1 whole, which is shorter than its diff:
```python
import functools
import math

import jax
import jax.numpy as jnp
from jax import lax
from jax.experimental import pallas as pl
from jax.experimental.pallas import tpu as pltpu
from jax.sharding import PartitionSpec as P

MESH = pl.DeviceIdType.MESH
VERY_LOW = -1e30
FLOOR = -1e29
KEY_PIECES = 8
VALUE_PIECES = ((1, 1, 1, 1), (2, 2, 2, 1, 1))
VALUE_LEAD = 0
PAUSE = 100


def attend(
    n,
    table_width,
    owners,
    pick_acc,
    score_acc,
    value_acc,
    q_hbm,
    k_hbm,
    v_hbm,
    pt_hbm,
    len_hbm,
    out_ref,
    q_raw,
    pt_vmem,
    len_smem,
    k_vmem,
    v_vmem,
    slot_seq,
    slot_live,
    picked,
    choose,
    soft,
    spread,
    bias,
    crest,
    row_vmem,
    row_smem,
    stat_out,
    stat_in,
    num_out,
    num_in,
    small_sem,
    k_sem,
    v_sem,
    stat_send,
    stat_recv,
    num_send,
    num_recv,
    fin_send,
    fin_recv,
):
    me = lax.axis_index("seq")
    batch, heads, head_dim = q_raw.shape
    slots, kv_heads, page, _ = k_vmem.shape
    pairs = kv_heads // 2
    half = heads // kv_heads
    rows = 2 * half
    pool = pt_vmem.shape[0]
    parts = len(owners)
    share = batch // parts
    f32, bf16 = jnp.float32, jnp.bfloat16
    factor = math.log2(math.e) / math.sqrt(head_dim)

    small = (
        pltpu.make_async_copy(pt_hbm, pt_vmem, small_sem.at[0]),
        pltpu.make_async_copy(len_hbm, len_smem, small_sem.at[1]),
        pltpu.make_async_copy(q_hbm, q_raw, small_sem.at[2]),
    )
    for copy in small:
        copy.start()
    pl.delay(PAUSE)
    span = slots // KEY_PIECES
    k_copies = [
        pltpu.make_async_copy(
            k_hbm.at[pl.ds(i * span, span)], k_vmem.at[pl.ds(i * span, span)], k_sem.at[i]
        )
        for i in range(KEY_PIECES)
    ]
    v_copies = []
    for j in range(pairs):
        cuts = VALUE_PIECES[min(j, 1)]
        unit, at = slots // sum(cuts), 0
        for size in cuts:
            pages = pl.ds(at, size * unit)
            v_copies.append(
                (
                    j,
                    at,
                    size * unit,
                    pltpu.make_async_copy(
                        v_hbm.at[pages, pl.ds(2 * j, 2)],
                        v_vmem.at[pages, pl.ds(2 * j, 2)],
                        v_sem.at[len(v_copies)],
                    ),
                )
            )
            at += size * unit
    for copy in k_copies:
        copy.start()
    unstarted = [copy for _, _, _, copy in v_copies]

    mine = functools.reduce(lambda a, b: a | b, [me == o for o in owners])
    rank = sum(jnp.where(me == o, i, 0) for i, o in enumerate(owners))
    barrier = pltpu.get_barrier_semaphore()

    @pl.when(mine)
    def _():
        for step in range(1, n):
            pl.semaphore_signal(
                barrier, inc=1, device_id={"seq": lax.rem(me + step, n)}, device_id_type=MESH
            )

    def stat_copy(i, slot):
        return pltpu.make_async_remote_copy(
            src_ref=stat_out.at[i],
            dst_ref=stat_in.at[slot],
            send_sem=stat_send.at[i],
            recv_sem=stat_recv.at[slot],
            device_id={"seq": owners[i]},
            device_id_type=MESH,
        )

    def num_copy(j, i, slot):
        return pltpu.make_async_remote_copy(
            src_ref=num_out.at[j, i],
            dst_ref=num_in.at[j, slot],
            send_sem=num_send.at[j, i],
            recv_sem=num_recv.at[j, slot],
            device_id={"seq": owners[i]},
            device_id_type=MESH,
        )

    def fin_copy(dest, i):
        block = out_ref.at[pl.ds(i * share, share)]
        return pltpu.make_async_remote_copy(
            src_ref=block,
            dst_ref=block,
            send_sem=fin_send.at[dest],
            recv_sem=fin_recv.at[i],
            device_id={"seq": dest},
            device_id_type=MESH,
        )

    def iota(shape, dim):
        return lax.broadcasted_iota(jnp.int32, shape, dim)

    small[0].wait()
    small[1].wait()
    entry = iota((1, pool), 1)
    live = jnp.zeros((1, pool), jnp.int32)
    owner_seq = jnp.zeros((1, pool), jnp.int32)
    for b in range(batch):
        past = entry >= b * table_width
        left = jnp.clip(len_smem[b] - page * (entry - b * table_width), 0, page)
        live = jnp.where(past, left, live)
        owner_seq = jnp.where(past, b, owner_seq)
    hit = pt_vmem[...].reshape(1, pool) == me * slots + iota((slots, pool), 0)
    seq_col = jnp.sum(jnp.where(hit, owner_seq.astype(f32), 0.0), axis=1, keepdims=True)
    live_col = jnp.sum(jnp.where(hit, live.astype(f32), 0.0), axis=1, keepdims=True)
    seq_wide = jnp.broadcast_to(seq_col, (slots, page))
    slot_seq[...] = seq_wide
    slot_live[...] = jnp.broadcast_to(live_col, (slots, page))
    lane = iota((rows, page), 1)
    lane_f = lane.astype(f32)
    diagonal = iota((slots, page), 0) == iota((slots, page), 1)
    seq_row = jnp.sum(jnp.where(diagonal, seq_wide, 0.0), axis=0, keepdims=True)
    seq_row = jnp.where(iota((1, page), 1) < slots, seq_row, -1.0)
    row_vmem[...] = jnp.clip(seq_row.astype(jnp.int32), 0, batch - 1)
    row_copy = pltpu.make_async_copy(row_vmem, row_smem, small_sem.at[3])
    row_copy.start()
    seq_row = jnp.broadcast_to(seq_row, (rows, page))

    small[2].wait()
    column = iota((heads, 2 * batch * heads), 1)
    line = iota((heads, 2 * batch * heads), 0)
    side = column // (batch * heads) == line % rows // half
    mark = jnp.where((column % heads == line) & side, column % (batch * heads) // heads, -1)
    mark = mark.astype(f32)
    queries = q_raw[...].reshape(batch * heads, head_dim)
    blank = jnp.zeros_like(queries)
    queries = jnp.concatenate(
        [
            jnp.concatenate([queries, blank], axis=1),
            jnp.concatenate([blank, queries], axis=1),
        ],
        axis=0,
    )
    for unit in range(2):
        pltpu.matmul_push_rhs(queries, staging_register=0, mxu_index=unit)
    group = slots // len(pick_acc)
    for i, acc in enumerate(pick_acc):
        pick = []
        for pp in range(i * group // 2, (i + 1) * group // 2):
            for j in range(pairs):
                for p in (2 * pp, 2 * pp + 1):
                    seq = slot_seq[p : p + 1, :]
                    seq = jnp.concatenate([seq, seq], axis=1)
                    pick.append(jnp.where(mark[j * rows : (j + 1) * rows] == seq, 1.0, 0.0))
        pick = jnp.concatenate(pick, axis=0).astype(bf16)
        pltpu.matmul_acc_lhs(acc, pick, load_staged_rhs=0 if i < 2 else None)
    for i, acc in enumerate(pick_acc):
        picked[i * group * heads : (i + 1) * group * heads, :] = pltpu.matmul_pop(acc).astype(bf16)

    wide = (iota((batch * rows, page), 0) // rows).astype(f32)
    each = iota((batch, page), 0).astype(f32)
    peaks = {(j, b): jnp.full((rows, page), VERY_LOW, f32) for j in range(pairs) for b in range(batch)}
    sums = [jnp.zeros((rows, page), f32) for _ in range(pairs)]

    def prepare(p):
        choose[p] = jnp.where(wide == slot_seq[p : p + 1, :], 1.0, 0.0).astype(bf16)
        bias[p] = jnp.where(each == slot_seq[p : p + 1, :], 0.0, VERY_LOW)

    def score(pp, j):
        both = [
            k_vmem[2 * pp : 2 * pp + 2, 2 * j + g].reshape(2 * page, head_dim) for g in range(2)
        ]
        tile = pp * pairs + j
        register = tile // 2 % 2
        pltpu.matmul_push_rhs(
            jnp.concatenate(both, axis=1),
            staging_register=register,
            mxu_index=tile % 2,
            transpose=True,
        )
        pltpu.matmul_acc_lhs(
            score_acc[tile],
            picked[tile * 2 * rows : (tile + 1) * 2 * rows, :],
            load_staged_rhs=register,
        )

    def scores(pp, j):
        found = pltpu.matmul_pop(score_acc[pp * pairs + j])
        return [found[i * rows : (i + 1) * rows, i * page : (i + 1) * page] for i in range(2)]

    def settle(p, j, s):
        s = jnp.where(lane_f < slot_live[p : p + 1, :], s * factor, VERY_LOW)
        soft[p, j] = s
        for b in range(batch):
            peaks[j, b] = jnp.maximum(peaks[j, b], s + bias[p, b : b + 1, :])

    for i in range(KEY_PIECES + 1):
        if i < KEY_PIECES:
            k_copies[i].wait()
            if i >= VALUE_LEAD:
                unstarted.pop(0).start()
            for pp in range(i * span // 2, (i + 1) * span // 2):
                for j in range(pairs):
                    score(pp, j)
            for p in range(i * span, (i + 1) * span):
                prepare(p)
        if i > 0:
            for pp in range((i - 1) * span // 2, i * span // 2):
                for j in range(pairs):
                    for k, found in enumerate(scores(pp, j)):
                        settle(2 * pp + k, j, found)

    row_copy.wait()
    for copy in unstarted:
        copy.start()
    for key in peaks:
        j, b = key
        peaks[key] = jnp.maximum(jnp.max(peaks[key], axis=1, keepdims=True), FLOOR)
        crest[b, j] = jnp.broadcast_to(peaks[key], (rows, page))

    def soften(j, p):
        seq = jnp.clip(row_smem[0, p], 0, batch - 1)
        w = jnp.exp2(soft[p, j] - crest[seq, j])
        sums[j] = jnp.where(lane == p, jnp.sum(w, axis=1, keepdims=True), sums[j])
        w = jnp.concatenate([w] * 2, axis=0).astype(bf16)
        w = jnp.concatenate([w] * (batch // 2), axis=0)
        spread[j, :, p * page : (p + 1) * page] = w * choose[p]

    stats = [jnp.zeros((rows, page), f32) for _ in range(parts)]
    inverse = {}

    def account(j):
        for b in range(batch):
            total = jnp.where(seq_row == float(b), sums[j], 0.0)
            total = jnp.sum(total, axis=1, keepdims=True)
            some = total > 0.0
            safe = jnp.where(some, total, 1.0)
            level = jnp.where(some, peaks[j, b] + jnp.log2(safe), VERY_LOW)
            inverse[j, b] = jnp.broadcast_to(1.0 / safe, (rows, head_dim))
            i, local = b // share, b % share
            stats[i] = jnp.where(lane == j * share + local, level, stats[i])

    upper = iota((batch * rows, head_dim), 0) % rows < half

    def gather(j, at, size):
        for pp in range(at // 2, (at + size) // 2):
            both = [
                v_vmem[2 * pp : 2 * pp + 2, 2 * j + g].reshape(2 * page, head_dim)
                for g in range(2)
            ]
            register = pp // 2 % 2
            pltpu.matmul_push_rhs(
                jnp.concatenate(both, axis=1), staging_register=register, mxu_index=pp % 2
            )
            pltpu.matmul_acc_lhs(
                value_acc[2 * j + pp % 2],
                spread[j, :, 2 * pp * page : 2 * (pp + 1) * page],
                load_staged_rhs=register,
            )

    def merge(j):
        found = pltpu.matmul_pop(value_acc[2 * j]) + pltpu.matmul_pop(value_acc[2 * j + 1])
        return jnp.where(upper, found[:, :head_dim], found[:, head_dim:])

    def post_stats():
        for i in range(parts):
            stat_out[i] = stats[i]
        pl.semaphore_wait(barrier, jnp.where(mine, parts - 1, parts))
        for i, o in enumerate(owners):
            @pl.when(me != o)
            def _():
                stat_copy(i, me).start()

            @pl.when(me == o)
            def _():
                stat_in[me] = stat_out[i]

    def post_numer(j, numer):
        scale = jnp.concatenate([inverse[j, b] for b in range(batch)], axis=0)
        num_out[j] = (numer * scale).astype(bf16).reshape(parts, share * rows, head_dim)
        for i, o in enumerate(owners):
            @pl.when(me != o)
            def _():
                num_copy(j, i, me).start()

            @pl.when(me == o)
            def _():
                num_in[j, me] = num_out[j, i]

    for p in range(slots):
        soften(0, p)
    owed = None
    for j, at, size, copy in v_copies:
        copy.wait()
        gather(j, at, size)
        if j == 0:
            if at == 0:
                account(0)
            for other in range(1, pairs):
                for p in range(at, at + size):
                    soften(other, p)
            if at + size == slots:
                for other in range(1, pairs):
                    account(other)
        if owed is not None:
            if owed == 0:
                post_stats()
            post_numer(owed, merge(owed))
        owed = j if at + size == slots else None
    post_numer(owed, merge(owed))

    @pl.when(mine)
    def _():
        for step in range(1, n):
            stat_copy(0, lax.rem(me + step, n)).wait_recv()
        levels = stat_in[...]
        scales = jnp.exp2(levels - jnp.max(levels, axis=0, keepdims=True))
        scales = scales / jnp.sum(scales, axis=0, keepdims=True)
        columns = {}
        for s in range(n):
            for at in range(pairs * share):
                columns[s, at] = jnp.broadcast_to(scales[s][:, at : at + 1], (rows, head_dim))
        blocks = []
        for j in range(pairs):
            for step in range(1, n):
                num_copy(j, 0, lax.rem(me + step, n)).wait_recv()
            for local in range(share):
                blocks.append(
                    sum(
                        columns[s, j * share + local]
                        * num_in[j, s, local * rows : (local + 1) * rows, :].astype(f32)
                        for s in range(n)
                    )
                )
        for local in range(share):
            whole = [blocks[j * share + local] for j in range(pairs)]
            out_ref[rank * share + local] = jnp.concatenate(whole, axis=0).astype(out_ref.dtype)
        for step in range(1, n):
            fin_copy(lax.rem(me + step, n), rank).start()

    for i, o in enumerate(owners):
        @pl.when(me != o)
        def _():
            stat_copy(i, me).wait_send()
            for j in range(pairs):
                num_copy(j, i, me).wait_send()
            fin_copy(o, i).wait_recv()

    @pl.when(mine)
    def _():
        for step in range(1, n):
            fin_copy(lax.rem(me + step, n), rank).wait_send()


def scoped(n, table_width, owners, batch, heads, slots, pairs, *refs):
    rows = heads // pairs
    pieces = 4
    accs = []
    for i in range(pieces):
        accs.append(pltpu.ACC(i % 2)((slots * heads // pieces, 256), jnp.float32))
    tiles = slots // 2 * pairs
    for i in range(tiles):
        accs.append(pltpu.ACC(i % 2)((2 * rows, 256), jnp.float32))
    for i in range(2 * pairs):
        accs.append(pltpu.ACC(i % 2)((batch * rows, 256), jnp.float32))

    def body(*accs):
        attend(
            n,
            table_width,
            owners,
            accs[:pieces],
            accs[pieces : pieces + tiles],
            accs[pieces + tiles :],
            *refs,
        )

    pl.run_scoped(body, *accs)


def shards(n, owners, query_rows, cache_keys, cache_values, page_table, seq_lengths):
    slots, kv_heads, page, head_dim = cache_keys.shape
    batch, heads, _ = query_rows.shape
    pool = page_table.shape[0]
    rows, pairs = 2 * heads // kv_heads, kv_heads // 2
    parts = len(owners)
    share = batch // parts
    f32, bf16 = jnp.float32, jnp.bfloat16
    hbm = pl.BlockSpec(memory_space=pl.ANY)
    dma = pltpu.SemaphoreType.DMA
    return pl.pallas_call(
        functools.partial(scoped, n, pool // batch, owners, batch, heads, slots, pairs),
        out_shape=pltpu.VMEM((batch, heads, head_dim), bf16),
        in_specs=[hbm] * 5,
        out_specs=pl.BlockSpec(memory_space=pltpu.VMEM),
        scratch_shapes=[
            pltpu.VMEM((batch, heads, head_dim), bf16),
            pltpu.VMEM((pool,), jnp.int32),
            pltpu.SMEM((batch,), jnp.int32),
            pltpu.VMEM((slots, kv_heads, page, head_dim), bf16),
            pltpu.VMEM((slots, kv_heads, page, head_dim), bf16),
            pltpu.VMEM((slots, page), f32),
            pltpu.VMEM((slots, page), f32),
            pltpu.VMEM((slots * heads, 2 * head_dim), bf16),
            pltpu.VMEM((slots, batch * rows, page), bf16),
            pltpu.VMEM((slots, pairs, rows, page), f32),
            pltpu.VMEM((pairs, batch * rows, slots * page), bf16),
            pltpu.VMEM((slots, batch, page), f32),
            pltpu.VMEM((batch, pairs, rows, page), f32),
            pltpu.VMEM((1, page), jnp.int32),
            pltpu.SMEM((1, page), jnp.int32),
            pltpu.VMEM((parts, rows, page), f32),
            pltpu.VMEM((n, rows, page), f32),
            pltpu.VMEM((pairs, parts, share * rows, head_dim), bf16),
            pltpu.VMEM((pairs, n, share * rows, head_dim), bf16),
            dma((4,)),
            dma((KEY_PIECES,)),
            dma((sum(len(VALUE_PIECES[min(j, 1)]) for j in range(pairs)),)),
            dma((parts,)),
            dma((n,)),
            dma((pairs, parts)),
            dma((pairs, n)),
            dma((n,)),
            dma((parts,)),
        ],
        compiler_params=pltpu.CompilerParams(collective_id=0, has_side_effects=True),
    )(query_rows, cache_keys, cache_values, page_table, seq_lengths)


def owners_of(n):
    return tuple(range(4))


def solution(mesh):
    n = mesh.shape["seq"]
    owners = owners_of(n)
    in_specs = (
        P("grp", "head", None),
        P(("grp", "seq"), "head", None, None),
        P(("grp", "seq"), "head", None, None),
        P("grp"),
        P("grp"),
    )
    return jax.shard_map(
        functools.partial(shards, n, owners),
        mesh=mesh,
        in_specs=in_specs,
        out_specs=P("grp", "head", None),
        check_vma=False,
    )
```

time: 17 us -> 15.4 us (0.906)
  Pallas kernels: 16.2 us -> 14.6 us
    pallas_call x1, Pallas kernels: 16.2 us -> 14.6 us  [shards(): pl.pallas_call(functools.partial(scoped, n, pool // batch, owners, batch,...]
    reshape x1 -> x0, local copies, waits for them, and re-layouts: 0.62 us -> none  [shards(): return out.reshape(heads, batch, head_dim).transpose(1, 0, 2)]
    unnamed x0 -> x1, local copies, waits for them, and re-layouts: none -> 0.62 us
where the time goes in v1:
time: 15.4 us; the launch traced here: 15.2 us
  Pallas kernels  14.6 us (95%)
  local copies, waits for them, and re-layouts  0.62 us (4%)
    pallas_call x1, Pallas kernels, shards(): pl.pallas_call(functools.partial(scoped, n, pool // batch, owners, batch,...  14.6 us
    unnamed x1, local copies, waits for them, and re-layouts  0.62 us

profile of v1, /device:TPU:0, one launch (start us, length us, event | category | flops | bytes accessed | tf_op | source)
XLA Modules:
  0.0 15.2 jit_solution(15197855555344525303)
XLA Ops:
  0.0 14.6 %shard_map.55 = bf16[8,16,128]{2,1,0:T(8,128)(2,1)S(1)} custom-call(bf16[8,16,128]{2,1,0:T(8,128)(2,1)} %refs_0_.1, bf16[32,4,128,128]{3,2,1,0:T(8,128)(2,1)} %refs_1_.1, bf16[32,4,128,128]{3,2,1,0:T(8,128)(2,1)} %refs_2_.1, s32[256]{0:T(256)} %refs_3_.1, s32[8]{0:T(128)} %refs_4_.1), custom_call_target="tpu_custom_call" | custom-call | tf_op jit(solution)/shard_map/pallas_call | solution.py:445
  14.6 0.6 %copy.7 = bf16[8,16,128]{2,1,0:T(8,128)(2,1)} copy(bf16[8,16,128]{2,1,0:T(8,128)(2,1)S(1)} %shard_map.55) | data formatting | bytes 65536

commit v2 on v1

--- a/solution.py
+++ b/solution.py
@@ -13,12 +13,14 @@
 FLOOR = -1e29
 KEY_PIECES = 8
 VALUE_PIECES = ((1, 1, 1, 1), (2, 2, 2, 1, 1))
-VALUE_LEAD = 0
+EARLY = 1
+STEP = 1
 PAUSE = 100
 
 
 def attend(
     n,
+    sides,
     table_width,
     owners,
     pick_acc,
@@ -45,6 +47,7 @@
     crest,
     row_vmem,
     row_smem,
+    done_ref,
     stat_out,
     stat_in,
     num_out,
@@ -60,6 +63,9 @@
     fin_recv,
 ):
     me = lax.axis_index("seq")
+    side = lax.axis_index("head")
+    gate = sides - 1
+    slot = side * n + me
     batch, heads, head_dim = q_raw.shape
     slots, kv_heads, page, _ = k_vmem.shape
     pairs = kv_heads // 2
@@ -108,16 +114,23 @@
     for copy in k_copies:
         copy.start()
     unstarted = [copy for _, _, _, copy in v_copies]
-
-    mine = functools.reduce(lambda a, b: a | b, [me == o for o in owners])
+    for _ in range(EARLY):
+        unstarted.pop(0).start()
+
+    mine = (side == gate) & functools.reduce(lambda a, b: a | b, [me == o for o in owners])
     rank = sum(jnp.where(me == o, i, 0) for i, o in enumerate(owners))
     barrier = pltpu.get_barrier_semaphore()
 
+    def others():
+        for h in range(sides):
+            for step in range(1 if h == gate else 0, n):
+                yield h, lax.rem(me + step, n)
+
     @pl.when(mine)
     def _():
-        for step in range(1, n):
+        for h, seq in others():
             pl.semaphore_signal(
-                barrier, inc=1, device_id={"seq": lax.rem(me + step, n)}, device_id_type=MESH
+                barrier, inc=1, device_id={"seq": seq, "head": h}, device_id_type=MESH
             )
 
     def stat_copy(i, slot):
@@ -126,7 +139,7 @@
             dst_ref=stat_in.at[slot],
             send_sem=stat_send.at[i],
             recv_sem=stat_recv.at[slot],
-            device_id={"seq": owners[i]},
+            device_id={"seq": owners[i], "head": gate},
             device_id_type=MESH,
         )
 
@@ -136,20 +149,25 @@
             dst_ref=num_in.at[j, slot],
             send_sem=num_send.at[j, i],
             recv_sem=num_recv.at[j, slot],
-            device_id={"seq": owners[i]},
+            device_id={"seq": owners[i], "head": gate},
             device_id_type=MESH,
         )
 
-    def fin_copy(dest, i):
-        block = out_ref.at[pl.ds(i * share, share)]
+    def fin_copy(h, seq, i):
         return pltpu.make_async_remote_copy(
-            src_ref=block,
-            dst_ref=block,
-            send_sem=fin_send.at[dest],
+            src_ref=done_ref.at[h],
+            dst_ref=out_ref.at[pl.ds(i * share, share)],
+            send_sem=fin_send.at[h, seq],
             recv_sem=fin_recv.at[i],
-            device_id={"seq": dest},
+            device_id={"seq": seq, "head": h},
             device_id_type=MESH,
         )
+
+    def own(o):
+        return (me == o) & (side == gate)
+
+    def foreign(o):
+        return (me != o) | (side != gate)
 
     def iota(shape, dim):
         return lax.broadcasted_iota(jnp.int32, shape, dim)
@@ -183,8 +201,8 @@
     small[2].wait()
     column = iota((heads, 2 * batch * heads), 1)
     line = iota((heads, 2 * batch * heads), 0)
-    side = column // (batch * heads) == line % rows // half
-    mark = jnp.where((column % heads == line) & side, column % (batch * heads) // heads, -1)
+    match = column // (batch * heads) == line % rows // half
+    mark = jnp.where((column % heads == line) & match, column % (batch * heads) // heads, -1)
     mark = mark.astype(f32)
     queries = q_raw[...].reshape(batch * heads, head_dim)
     blank = jnp.zeros_like(queries)
@@ -251,7 +269,7 @@
     for i in range(KEY_PIECES + 1):
         if i < KEY_PIECES:
             k_copies[i].wait()
-            if i >= VALUE_LEAD:
+            for _ in range(min(STEP, len(unstarted))):
                 unstarted.pop(0).start()
             for pp in range(i * span // 2, (i + 1) * span // 2):
                 for j in range(pairs):
@@ -321,25 +339,25 @@
             stat_out[i] = stats[i]
         pl.semaphore_wait(barrier, jnp.where(mine, parts - 1, parts))
         for i, o in enumerate(owners):
-            @pl.when(me != o)
+            @pl.when(foreign(o))
             def _():
-                stat_copy(i, me).start()
-
-            @pl.when(me == o)
+                stat_copy(i, slot).start()
+
+            @pl.when(own(o))
             def _():
-                stat_in[me] = stat_out[i]
+                stat_in[slot] = stat_out[i]
 
     def post_numer(j, numer):
         scale = jnp.concatenate([inverse[j, b] for b in range(batch)], axis=0)
-        num_out[j] = (numer * scale).astype(bf16).reshape(parts, share * rows, head_dim)
+        num_out[j] = (numer * scale).reshape(parts, share * rows, head_dim)
         for i, o in enumerate(owners):
-            @pl.when(me != o)
+            @pl.when(foreign(o))
             def _():
-                num_copy(j, i, me).start()
-
-            @pl.when(me == o)
+                num_copy(j, i, slot).start()
+
+            @pl.when(own(o))
             def _():
-                num_in[j, me] = num_out[j, i]
+                num_in[j, slot] = num_out[j, i]
 
     for p in range(slots):
         soften(0, p)
@@ -365,48 +383,58 @@
 
     @pl.when(mine)
     def _():
-        for step in range(1, n):
-            stat_copy(0, lax.rem(me + step, n)).wait_recv()
-        levels = stat_in[...]
-        scales = jnp.exp2(levels - jnp.max(levels, axis=0, keepdims=True))
-        scales = scales / jnp.sum(scales, axis=0, keepdims=True)
         columns = {}
-        for s in range(n):
-            for at in range(pairs * share):
-                columns[s, at] = jnp.broadcast_to(scales[s][:, at : at + 1], (rows, head_dim))
-        blocks = []
-        for j in range(pairs):
-            for step in range(1, n):
-                num_copy(j, 0, lax.rem(me + step, n)).wait_recv()
+        for h in range(sides):
+            for other, seq in others():
+                if other == h:
+                    stat_copy(0, h * n + seq).wait_recv()
+            levels = stat_in[h * n : (h + 1) * n]
+            scales = jnp.exp2(levels - jnp.max(levels, axis=0, keepdims=True))
+            scales = scales / jnp.sum(scales, axis=0, keepdims=True)
+            for s in range(n):
+                for at in range(pairs * share):
+                    columns[h, s, at] = jnp.broadcast_to(
+                        scales[s][:, at : at + 1], (rows, head_dim)
+                    )
+        for h in range(sides):
+            blocks = []
+            for j in range(pairs):
+                for other, seq in others():
+                    if other == h:
+                        num_copy(j, 0, h * n + seq).wait_recv()
+                for local in range(share):
+                    blocks.append(
+                        sum(
+                            columns[h, s, j * share + local]
+                            * num_in[j, h * n + s, local * rows : (local + 1) * rows, :]
+                            for s in range(n)
+                        )
+                    )
             for local in range(share):
-                blocks.append(
-                    sum(
-                        columns[s, j * share + local]
-                        * num_in[j, s, local * rows : (local + 1) * rows, :].astype(f32)
-                        for s in range(n)
-                    )
-                )
-        for local in range(share):
-            whole = [blocks[j * share + local] for j in range(pairs)]
-            out_ref[rank * share + local] = jnp.concatenate(whole, axis=0).astype(out_ref.dtype)
-        for step in range(1, n):
-            fin_copy(lax.rem(me + step, n), rank).start()
+                whole = [blocks[j * share + local] for j in range(pairs)]
+                whole = jnp.concatenate(whole, axis=0).astype(out_ref.dtype)
+                done_ref[h, local] = whole
+                if h == gate:
+                    out_ref[rank * share + local] = whole
+            for other, seq in others():
+                if other == h:
+                    fin_copy(h, seq, rank).start()
 
     for i, o in enumerate(owners):
-        @pl.when(me != o)
+        @pl.when(foreign(o))
         def _():
-            stat_copy(i, me).wait_send()
+            stat_copy(i, slot).wait_send()
             for j in range(pairs):
-                num_copy(j, i, me).wait_send()
-            fin_copy(o, i).wait_recv()
+                num_copy(j, i, slot).wait_send()
+            fin_copy(0, o, i).wait_recv()
 
     @pl.when(mine)
     def _():
-        for step in range(1, n):
-            fin_copy(lax.rem(me + step, n), rank).wait_send()
-
-
-def scoped(n, table_width, owners, batch, heads, slots, pairs, *refs):
+        for h, seq in others():
+            fin_copy(h, seq, rank).wait_send()
+
+
+def scoped(n, sides, table_width, owners, batch, heads, slots, pairs, *refs):
     rows = heads // pairs
     pieces = 4
     accs = []
@@ -421,6 +449,7 @@
     def body(*accs):
         attend(
             n,
+            sides,
             table_width,
             owners,
             accs[:pieces],
@@ -432,7 +461,7 @@
     pl.run_scoped(body, *accs)
 
 
-def shards(n, owners, query_rows, cache_keys, cache_values, page_table, seq_lengths):
+def shards(n, sides, owners, query_rows, cache_keys, cache_values, page_table, seq_lengths):
     slots, kv_heads, page, head_dim = cache_keys.shape
     batch, heads, _ = query_rows.shape
     pool = page_table.shape[0]
@@ -443,7 +472,7 @@
     hbm = pl.BlockSpec(memory_space=pl.ANY)
     dma = pltpu.SemaphoreType.DMA
     return pl.pallas_call(
-        functools.partial(scoped, n, pool // batch, owners, batch, heads, slots, pairs),
+        functools.partial(scoped, n, sides, pool // batch, owners, batch, heads, slots, pairs),
         out_shape=pltpu.VMEM((batch, heads, head_dim), bf16),
         in_specs=[hbm] * 5,
         out_specs=pl.BlockSpec(memory_space=pltpu.VMEM),
@@ -463,18 +492,19 @@
             pltpu.VMEM((batch, pairs, rows, page), f32),
             pltpu.VMEM((1, page), jnp.int32),
             pltpu.SMEM((1, page), jnp.int32),
+            pltpu.VMEM((sides, share, heads, head_dim), bf16),
             pltpu.VMEM((parts, rows, page), f32),
-            pltpu.VMEM((n, rows, page), f32),
-            pltpu.VMEM((pairs, parts, share * rows, head_dim), bf16),
-            pltpu.VMEM((pairs, n, share * rows, head_dim), bf16),
+            pltpu.VMEM((sides * n, rows, page), f32),
+            pltpu.VMEM((pairs, parts, share * rows, head_dim), f32),
+            pltpu.VMEM((pairs, sides * n, share * rows, head_dim), f32),
             dma((4,)),
             dma((KEY_PIECES,)),
             dma((sum(len(VALUE_PIECES[min(j, 1)]) for j in range(pairs)),)),
             dma((parts,)),
-            dma((n,)),
+            dma((sides * n,)),
             dma((pairs, parts)),
-            dma((pairs, n)),
-            dma((n,)),
+            dma((pairs, sides * n)),
+            dma((sides, n)),
             dma((parts,)),
         ],
         compiler_params=pltpu.CompilerParams(collective_id=0, has_side_effects=True),
@@ -482,7 +512,7 @@
 
 
 def owners_of(n):
-    return tuple(range(4))
+    return tuple(range(n // 2 - 2, n // 2 + 2))
 
 
 def solution(mesh):
@@ -496,7 +526,7 @@
         P("grp"),
     )
     return jax.shard_map(
-        functools.partial(shards, n, owners),
+        functools.partial(shards, n, mesh.shape["head"], owners),
         mesh=mesh,
         in_specs=in_specs,
         out_specs=P("grp", "head", None),

time: 15.4 us -> 15 us (0.974)
  Pallas kernels: 14.6 us -> 14.2 us
    pallas_call x1, Pallas kernels: 14.6 us -> 14.2 us  [shards(): pl.pallas_call(functools.partial(scoped, n, sides, pool // batch, owners,...]
where the time goes in v2:
time: 15 us; the launch traced here: 14.8 us
  Pallas kernels  14.2 us (95%)
  local copies, waits for them, and re-layouts  0.62 us (4%)
    pallas_call x1, Pallas kernels, shards(): pl.pallas_call(functools.partial(scoped, n, sides, pool // batch, owners,...  14.2 us
    unnamed x1, local copies, waits for them, and re-layouts  0.62 us

profile of v2, /device:TPU:0, one launch (start us, length us, event | category | flops | bytes accessed | tf_op | source)
XLA Modules:
  0.0 14.8 jit_solution(16590524926704332319)
XLA Ops:
  0.0 14.2 %shard_map.55 = bf16[8,16,128]{2,1,0:T(8,128)(2,1)S(1)} custom-call(bf16[8,16,128]{2,1,0:T(8,128)(2,1)} %refs_0_.1, bf16[32,4,128,128]{3,2,1,0:T(8,128)(2,1)} %refs_1_.1, bf16[32,4,128,128]{3,2,1,0:T(8,128)(2,1)} %refs_2_.1, s32[256]{0:T(256)} %refs_3_.1, s32[8]{0:T(128)} %refs_4_.1), custom_call_target="tpu_custom_call" | custom-call | tf_op jit(solution)/shard_map/pallas_call | solution.py:474
  14.2 0.6 %copy.7 = bf16[8,16,128]{2,1,0:T(8,128)(2,1)} copy(bf16[8,16,128]{2,1,0:T(8,128)(2,1)S(1)} %shard_map.55) | data formatting | bytes 65536

commit v3 on v2

--- a/solution.py
+++ b/solution.py
@@ -48,6 +48,7 @@
     row_vmem,
     row_smem,
     done_ref,
+    tally,
     stat_out,
     stat_in,
     num_out,
@@ -106,7 +107,9 @@
                     pltpu.make_async_copy(
                         v_hbm.at[pages, pl.ds(2 * j, 2)],
                         v_vmem.at[pages, pl.ds(2 * j, 2)],
-                        v_sem.at[len(v_copies)],
+                        v_sem.at[len(v_copies)]
+                        if len(v_copies) < EARLY
+                        else k_sem.at[len(v_copies) - EARLY],
                     ),
                 )
             )
@@ -133,22 +136,22 @@
                 barrier, inc=1, device_id={"seq": seq, "head": h}, device_id_type=MESH
             )
 
-    def stat_copy(i, slot):
+    def stat_copy(i):
         return pltpu.make_async_remote_copy(
             src_ref=stat_out.at[i],
             dst_ref=stat_in.at[slot],
-            send_sem=stat_send.at[i],
-            recv_sem=stat_recv.at[slot],
+            send_sem=stat_send,
+            recv_sem=stat_recv.at[side],
             device_id={"seq": owners[i], "head": gate},
             device_id_type=MESH,
         )
 
-    def num_copy(j, i, slot):
+    def num_copy(j, i):
         return pltpu.make_async_remote_copy(
             src_ref=num_out.at[j, i],
             dst_ref=num_in.at[j, slot],
-            send_sem=num_send.at[j, i],
-            recv_sem=num_recv.at[j, slot],
+            send_sem=num_send,
+            recv_sem=num_recv.at[j, side],
             device_id={"seq": owners[i], "head": gate},
             device_id_type=MESH,
         )
@@ -157,17 +160,24 @@
         return pltpu.make_async_remote_copy(
             src_ref=done_ref.at[h],
             dst_ref=out_ref.at[pl.ds(i * share, share)],
-            send_sem=fin_send.at[h, seq],
-            recv_sem=fin_recv.at[i],
+            send_sem=fin_send,
+            recv_sem=fin_recv,
             device_id={"seq": seq, "head": h},
             device_id_type=MESH,
         )
 
+    def bytes_of(ref, sem):
+        return pltpu.make_async_remote_copy(
+            src_ref=ref,
+            dst_ref=ref,
+            send_sem=sem,
+            recv_sem=sem,
+            device_id={"seq": owners[0], "head": gate},
+            device_id_type=MESH,
+        )
+
     def own(o):
         return (me == o) & (side == gate)
-
-    def foreign(o):
-        return (me != o) | (side != gate)
 
     def iota(shape, dim):
         return lax.broadcasted_iota(jnp.int32, shape, dim)
@@ -194,7 +204,7 @@
     seq_row = jnp.sum(jnp.where(diagonal, seq_wide, 0.0), axis=0, keepdims=True)
     seq_row = jnp.where(iota((1, page), 1) < slots, seq_row, -1.0)
     row_vmem[...] = jnp.clip(seq_row.astype(jnp.int32), 0, batch - 1)
-    row_copy = pltpu.make_async_copy(row_vmem, row_smem, small_sem.at[3])
+    row_copy = pltpu.make_async_copy(row_vmem, row_smem, small_sem.at[0])
     row_copy.start()
     seq_row = jnp.broadcast_to(seq_row, (rows, page))
 
@@ -226,9 +236,13 @@
                     pick.append(jnp.where(mark[j * rows : (j + 1) * rows] == seq, 1.0, 0.0))
         pick = jnp.concatenate(pick, axis=0).astype(bf16)
         pltpu.matmul_acc_lhs(acc, pick, load_staged_rhs=0 if i < 2 else None)
-    for i, acc in enumerate(pick_acc):
-        picked[i * group * heads : (i + 1) * group * heads, :] = pltpu.matmul_pop(acc).astype(bf16)
-
+    def store_picks(i):
+        found = pltpu.matmul_pop(pick_acc[i]).astype(bf16)
+        here = pl.ds(i * group * heads, group * heads)
+        picked[0, here] = found[:, :head_dim]
+        picked[1, here] = found[:, head_dim:]
+
+    store_picks(0)
     wide = (iota((batch * rows, page), 0) // rows).astype(f32)
     each = iota((batch, page), 0).astype(f32)
     peaks = {(j, b): jnp.full((rows, page), VERY_LOW, f32) for j in range(pairs) for b in range(batch)}
@@ -252,7 +266,7 @@
         )
         pltpu.matmul_acc_lhs(
             score_acc[tile],
-            picked[tile * 2 * rows : (tile + 1) * 2 * rows, :],
+            jnp.concatenate([picked[g, pl.ds(tile * 2 * rows, 2 * rows)] for g in range(2)], axis=1),
             load_staged_rhs=register,
         )
 
@@ -274,6 +288,8 @@
             for pp in range(i * span // 2, (i + 1) * span // 2):
                 for j in range(pairs):
                     score(pp, j)
+            if i + 1 < KEY_PIECES:
+                store_picks(i + 1)
             for p in range(i * span, (i + 1) * span):
                 prepare(p)
         if i > 0:
@@ -296,7 +312,7 @@
         sums[j] = jnp.where(lane == p, jnp.sum(w, axis=1, keepdims=True), sums[j])
         w = jnp.concatenate([w] * 2, axis=0).astype(bf16)
         w = jnp.concatenate([w] * (batch // 2), axis=0)
-        spread[j, :, p * page : (p + 1) * page] = w * choose[p]
+        spread[j, p] = w * choose[p]
 
     stats = [jnp.zeros((rows, page), f32) for _ in range(parts)]
     inverse = {}
@@ -326,23 +342,33 @@
             )
             pltpu.matmul_acc_lhs(
                 value_acc[2 * j + pp % 2],
-                spread[j, :, 2 * pp * page : 2 * (pp + 1) * page],
+                jnp.concatenate([spread[j, 2 * pp], spread[j, 2 * pp + 1]], axis=1),
                 load_staged_rhs=register,
             )
 
     def merge(j):
         found = pltpu.matmul_pop(value_acc[2 * j]) + pltpu.matmul_pop(value_acc[2 * j + 1])
         return jnp.where(upper, found[:, :head_dim], found[:, head_dim:])
+
+    def post(start):
+        @pl.when(jnp.logical_not(mine))
+        def _():
+            for i in range(parts):
+                start(i)
+
+        @pl.when(mine)
+        def _():
+            for i, o in enumerate(owners):
+                @pl.when(me != o)
+                def _():
+                    start(i)
 
     def post_stats():
         for i in range(parts):
             stat_out[i] = stats[i]
         pl.semaphore_wait(barrier, jnp.where(mine, parts - 1, parts))
+        post(lambda i: stat_copy(i).start())
         for i, o in enumerate(owners):
-            @pl.when(foreign(o))
-            def _():
-                stat_copy(i, slot).start()
-
             @pl.when(own(o))
             def _():
                 stat_in[slot] = stat_out[i]
@@ -350,29 +376,27 @@
     def post_numer(j, numer):
         scale = jnp.concatenate([inverse[j, b] for b in range(batch)], axis=0)
         num_out[j] = (numer * scale).reshape(parts, share * rows, head_dim)
+        post(lambda i: num_copy(j, i).start())
         for i, o in enumerate(owners):
-            @pl.when(foreign(o))
-            def _():
-                num_copy(j, i, slot).start()
-
             @pl.when(own(o))
             def _():
                 num_in[j, slot] = num_out[j, i]
 
-    for p in range(slots):
+    first = v_copies[0][2]
+    for p in range(first):
         soften(0, p)
     owed = None
     for j, at, size, copy in v_copies:
         copy.wait()
         gather(j, at, size)
         if j == 0:
-            if at == 0:
-                account(0)
+            for p in range(at + size, min(at + size + first, slots)):
+                soften(0, p)
             for other in range(1, pairs):
                 for p in range(at, at + size):
                     soften(other, p)
             if at + size == slots:
-                for other in range(1, pairs):
+                for other in range(pairs):
                     account(other)
         if owed is not None:
             if owed == 0:
@@ -385,9 +409,8 @@
     def _():
         columns = {}
         for h in range(sides):
-            for other, seq in others():
-                if other == h:
-                    stat_copy(0, h * n + seq).wait_recv()
+            senders = n - 1 if h == gate else n
+            bytes_of(stat_in.at[pl.ds(0, senders)], stat_recv.at[h]).wait_recv()
             levels = stat_in[h * n : (h + 1) * n]
             scales = jnp.exp2(levels - jnp.max(levels, axis=0, keepdims=True))
             scales = scales / jnp.sum(scales, axis=0, keepdims=True)
@@ -397,11 +420,10 @@
                         scales[s][:, at : at + 1], (rows, head_dim)
                     )
         for h in range(sides):
+            senders = n - 1 if h == gate else n
             blocks = []
             for j in range(pairs):
-                for other, seq in others():
-                    if other == h:
-                        num_copy(j, 0, h * n + seq).wait_recv()
+                bytes_of(num_in.at[j, pl.ds(0, senders)], num_recv.at[j, h]).wait_recv()
                 for local in range(share):
                     blocks.append(
                         sum(
@@ -420,23 +442,24 @@
                 if other == h:
                     fin_copy(h, seq, rank).start()
 
-    for i, o in enumerate(owners):
-        @pl.when(foreign(o))
-        def _():
-            stat_copy(i, slot).wait_send()
-            for j in range(pairs):
-                num_copy(j, i, slot).wait_send()
-            fin_copy(0, o, i).wait_recv()
+    @pl.when(jnp.logical_not(mine))
+    def _():
+        bytes_of(stat_out, stat_send).wait_send()
+        bytes_of(num_out, num_send).wait_send()
+        bytes_of(out_ref, fin_recv).wait_recv()
 
     @pl.when(mine)
     def _():
-        for h, seq in others():
-            fin_copy(h, seq, rank).wait_send()
+        if parts > 1:
+            bytes_of(stat_out.at[pl.ds(0, parts - 1)], stat_send).wait_send()
+            bytes_of(num_out.at[:, pl.ds(0, parts - 1)], num_send).wait_send()
+            bytes_of(out_ref.at[pl.ds(0, (parts - 1) * share)], fin_recv).wait_recv()
+        bytes_of(tally, fin_send).wait_send()
 
 
 def scoped(n, sides, table_width, owners, batch, heads, slots, pairs, *refs):
     rows = heads // pairs
-    pieces = 4
+    pieces = KEY_PIECES
     accs = []
     for i in range(pieces):
         accs.append(pltpu.ACC(i % 2)((slots * heads // pieces, 256), jnp.float32))
@@ -484,28 +507,29 @@
             pltpu.VMEM((slots, kv_heads, page, head_dim), bf16),
             pltpu.VMEM((slots, page), f32),
             pltpu.VMEM((slots, page), f32),
-            pltpu.VMEM((slots * heads, 2 * head_dim), bf16),
+            pltpu.VMEM((2, slots * heads, head_dim), bf16),
             pltpu.VMEM((slots, batch * rows, page), bf16),
             pltpu.VMEM((slots, pairs, rows, page), f32),
-            pltpu.VMEM((pairs, batch * rows, slots * page), bf16),
+            pltpu.VMEM((pairs, slots, batch * rows, page), bf16),
             pltpu.VMEM((slots, batch, page), f32),
             pltpu.VMEM((batch, pairs, rows, page), f32),
             pltpu.VMEM((1, page), jnp.int32),
             pltpu.SMEM((1, page), jnp.int32),
             pltpu.VMEM((sides, share, heads, head_dim), bf16),
+            pltpu.VMEM((sides * n - 1, share, heads, head_dim), bf16),
             pltpu.VMEM((parts, rows, page), f32),
             pltpu.VMEM((sides * n, rows, page), f32),
             pltpu.VMEM((pairs, parts, share * rows, head_dim), f32),
             pltpu.VMEM((pairs, sides * n, share * rows, head_dim), f32),
-            dma((4,)),
+            dma((3,)),
             dma((KEY_PIECES,)),
-            dma((sum(len(VALUE_PIECES[min(j, 1)]) for j in range(pairs)),)),
-            dma((parts,)),
-            dma((sides * n,)),
-            dma((pairs, parts)),
-            dma((pairs, sides * n)),
-            dma((sides, n)),
-            dma((parts,)),
+            dma((EARLY,)),
+            dma,
+            dma((sides,)),
+            dma,
+            dma((pairs, sides)),
+            dma,
+            dma,
         ],
         compiler_params=pltpu.CompilerParams(collective_id=0, has_side_effects=True),
     )(query_rows, cache_keys, cache_values, page_table, seq_lengths)

time: 15 us -> 14.3 us (0.953)
  Pallas kernels: 14.2 us -> 13.5 us
    pallas_call x1, Pallas kernels: 14.2 us -> 13.5 us  [shards(): pl.pallas_call(functools.partial(scoped, n, sides, pool // batch, owners,...]
where the time goes in v3:
time: 14.3 us; the launch traced here: 14.1 us
  Pallas kernels  13.5 us (94%)
  local copies, waits for them, and re-layouts  0.62 us (4%)
    pallas_call x1, Pallas kernels, shards(): pl.pallas_call(functools.partial(scoped, n, sides, pool // batch, owners,...  13.5 us
    unnamed x1, local copies, waits for them, and re-layouts  0.62 us

profile of v3, /device:TPU:0, one launch (start us, length us, event | category | flops | bytes accessed | tf_op | source)
XLA Modules:
  0.0 14.1 jit_solution(4706164459155546402)
XLA Ops:
  0.0 13.5 %shard_map.55 = bf16[8,16,128]{2,1,0:T(8,128)(2,1)S(1)} custom-call(bf16[8,16,128]{2,1,0:T(8,128)(2,1)} %refs_0_.1, bf16[32,4,128,128]{3,2,1,0:T(8,128)(2,1)} %refs_1_.1, bf16[32,4,128,128]{3,2,1,0:T(8,128)(2,1)} %refs_2_.1, s32[256]{0:T(256)} %refs_3_.1, s32[8]{0:T(128)} %refs_4_.1), custom_call_target="tpu_custom_call" | custom-call | tf_op jit(solution)/shard_map/pallas_call | solution.py:497
  13.5 0.6 %copy.7 = bf16[8,16,128]{2,1,0:T(8,128)(2,1)} copy(bf16[8,16,128]{2,1,0:T(8,128)(2,1)S(1)} %shard_map.55) | data formatting | bytes 65536

commit v4 on v3

--- a/solution.py
+++ b/solution.py
@@ -15,7 +15,7 @@
 VALUE_PIECES = ((1, 1, 1, 1), (2, 2, 2, 1, 1))
 EARLY = 1
 STEP = 1
-PAUSE = 100
+PAUSE = 40
 
 
 def attend(
@@ -66,15 +66,12 @@
     me = lax.axis_index("seq")
     side = lax.axis_index("head")
     gate = sides - 1
-    slot = side * n + me
     batch, heads, head_dim = q_raw.shape
     slots, kv_heads, page, _ = k_vmem.shape
     pairs = kv_heads // 2
     half = heads // kv_heads
     rows = 2 * half
     pool = pt_vmem.shape[0]
-    parts = len(owners)
-    share = batch // parts
     f32, bf16 = jnp.float32, jnp.bfloat16
     factor = math.log2(math.e) / math.sqrt(head_dim)
 
@@ -120,46 +117,55 @@
     for _ in range(EARLY):
         unstarted.pop(0).start()
 
-    mine = (side == gate) & functools.reduce(lambda a, b: a | b, [me == o for o in owners])
-    rank = sum(jnp.where(me == o, i, 0) for i, o in enumerate(owners))
+    serves = [
+        (side == gate) & functools.reduce(lambda a, b: a | b, [me == o for o in owners[h]])
+        for h in range(sides)
+    ]
+    mine = serves[gate]
+    parts = len(owners[0])
+    share = batch // parts
+    rank = sum(jnp.where(me == o, i, 0) for h in range(sides) for i, o in enumerate(owners[h]))
+    targets = [
+        sum(jnp.where(side == h, owners[h][i], 0) for h in range(sides)) for i in range(parts)
+    ]
     barrier = pltpu.get_barrier_semaphore()
 
-    def others():
-        for h in range(sides):
-            for step in range(1 if h == gate else 0, n):
-                yield h, lax.rem(me + step, n)
-
-    @pl.when(mine)
-    def _():
-        for h, seq in others():
-            pl.semaphore_signal(
-                barrier, inc=1, device_id={"seq": seq, "head": h}, device_id_type=MESH
-            )
+    def members(h):
+        for seq in range(n - 1 if h == gate else n):
+            yield jnp.where(me <= seq, seq + 1, seq) if h == gate else seq
+
+    for h in range(sides):
+        @pl.when(serves[h])
+        def _():
+            for seq in members(h):
+                pl.semaphore_signal(
+                    barrier, inc=1, device_id={"seq": seq, "head": h}, device_id_type=MESH
+                )
 
     def stat_copy(i):
         return pltpu.make_async_remote_copy(
             src_ref=stat_out.at[i],
-            dst_ref=stat_in.at[slot],
+            dst_ref=stat_in.at[me],
             send_sem=stat_send,
-            recv_sem=stat_recv.at[side],
-            device_id={"seq": owners[i], "head": gate},
+            recv_sem=stat_recv,
+            device_id={"seq": targets[i], "head": gate},
             device_id_type=MESH,
         )
 
     def num_copy(j, i):
         return pltpu.make_async_remote_copy(
             src_ref=num_out.at[j, i],
-            dst_ref=num_in.at[j, slot],
+            dst_ref=num_in.at[j, me],
             send_sem=num_send,
-            recv_sem=num_recv.at[j, side],
-            device_id={"seq": owners[i], "head": gate},
+            recv_sem=num_recv.at[j],
+            device_id={"seq": targets[i], "head": gate},
             device_id_type=MESH,
         )
 
-    def fin_copy(h, seq, i):
+    def fin_copy(h, seq):
         return pltpu.make_async_remote_copy(
-            src_ref=done_ref.at[h],
-            dst_ref=out_ref.at[pl.ds(i * share, share)],
+            src_ref=done_ref,
+            dst_ref=out_ref.at[pl.ds(rank * share, share)],
             send_sem=fin_send,
             recv_sem=fin_recv,
             device_id={"seq": seq, "head": h},
@@ -172,12 +178,9 @@
             dst_ref=ref,
             send_sem=sem,
             recv_sem=sem,
-            device_id={"seq": owners[0], "head": gate},
+            device_id={"seq": targets[0], "head": gate},
             device_id_type=MESH,
         )
-
-    def own(o):
-        return (me == o) & (side == gate)
 
     def iota(shape, dim):
         return lax.broadcasted_iota(jnp.int32, shape, dim)
@@ -350,7 +353,7 @@
         found = pltpu.matmul_pop(value_acc[2 * j]) + pltpu.matmul_pop(value_acc[2 * j + 1])
         return jnp.where(upper, found[:, :head_dim], found[:, head_dim:])
 
-    def post(start):
+    def post(start, keep):
         @pl.when(jnp.logical_not(mine))
         def _():
             for i in range(parts):
@@ -358,29 +361,33 @@
 
         @pl.when(mine)
         def _():
-            for i, o in enumerate(owners):
+            for i, o in enumerate(owners[gate]):
                 @pl.when(me != o)
                 def _():
                     start(i)
+
+                @pl.when(me == o)
+                def _():
+                    keep(i)
 
     def post_stats():
         for i in range(parts):
             stat_out[i] = stats[i]
         pl.semaphore_wait(barrier, jnp.where(mine, parts - 1, parts))
-        post(lambda i: stat_copy(i).start())
-        for i, o in enumerate(owners):
-            @pl.when(own(o))
-            def _():
-                stat_in[slot] = stat_out[i]
+
+        def keep(i):
+            stat_in[me] = stat_out[i]
+
+        post(lambda i: stat_copy(i).start(), keep)
 
     def post_numer(j, numer):
         scale = jnp.concatenate([inverse[j, b] for b in range(batch)], axis=0)
         num_out[j] = (numer * scale).reshape(parts, share * rows, head_dim)
-        post(lambda i: num_copy(j, i).start())
-        for i, o in enumerate(owners):
-            @pl.when(own(o))
-            def _():
-                num_in[j, slot] = num_out[j, i]
+
+        def keep(i):
+            num_in[j, me] = num_out[j, i]
+
+        post(lambda i: num_copy(j, i).start(), keep)
 
     first = v_copies[0][2]
     for p in range(first):
@@ -405,42 +412,37 @@
         owed = j if at + size == slots else None
     post_numer(owed, merge(owed))
 
-    @pl.when(mine)
-    def _():
+    def combine(h):
+        senders = n - 1 if h == gate else n
+        bytes_of(stat_in.at[pl.ds(0, senders)], stat_recv).wait_recv()
+        levels = stat_in[...]
+        scales = jnp.exp2(levels - jnp.max(levels, axis=0, keepdims=True))
+        scales = scales / jnp.sum(scales, axis=0, keepdims=True)
         columns = {}
-        for h in range(sides):
-            senders = n - 1 if h == gate else n
-            bytes_of(stat_in.at[pl.ds(0, senders)], stat_recv.at[h]).wait_recv()
-            levels = stat_in[h * n : (h + 1) * n]
-            scales = jnp.exp2(levels - jnp.max(levels, axis=0, keepdims=True))
-            scales = scales / jnp.sum(scales, axis=0, keepdims=True)
-            for s in range(n):
-                for at in range(pairs * share):
-                    columns[h, s, at] = jnp.broadcast_to(
-                        scales[s][:, at : at + 1], (rows, head_dim)
-                    )
-        for h in range(sides):
-            senders = n - 1 if h == gate else n
-            blocks = []
-            for j in range(pairs):
-                bytes_of(num_in.at[j, pl.ds(0, senders)], num_recv.at[j, h]).wait_recv()
-                for local in range(share):
-                    blocks.append(
-                        sum(
-                            columns[h, s, j * share + local]
-                            * num_in[j, h * n + s, local * rows : (local + 1) * rows, :]
-                            for s in range(n)
-                        )
-                    )
+        for s in range(n):
+            for at in range(pairs * share):
+                columns[s, at] = jnp.broadcast_to(scales[s][:, at : at + 1], (rows, head_dim))
+        blocks = []
+        for j in range(pairs):
+            bytes_of(num_in.at[j, pl.ds(0, senders)], num_recv.at[j]).wait_recv()
             for local in range(share):
-                whole = [blocks[j * share + local] for j in range(pairs)]
-                whole = jnp.concatenate(whole, axis=0).astype(out_ref.dtype)
-                done_ref[h, local] = whole
-                if h == gate:
-                    out_ref[rank * share + local] = whole
-            for other, seq in others():
-                if other == h:
-                    fin_copy(h, seq, rank).start()
+                here = pl.ds(local * rows, rows)
+                blocks.append(
+                    sum(columns[s, j * share + local] * num_in[j, s, here, :] for s in range(n))
+                )
+        for local in range(share):
+            whole = [blocks[j * share + local] for j in range(pairs)]
+            whole = jnp.concatenate(whole, axis=0).astype(out_ref.dtype)
+            done_ref[local] = whole
+            if h == gate:
+                out_ref[rank * share + local] = whole
+        for seq in members(h):
+            fin_copy(h, seq).start()
+
+    for h in range(sides):
+        @pl.when(serves[h])
+        def _():
+            combine(h)
 
     @pl.when(jnp.logical_not(mine))
     def _():
@@ -454,7 +456,11 @@
             bytes_of(stat_out.at[pl.ds(0, parts - 1)], stat_send).wait_send()
             bytes_of(num_out.at[:, pl.ds(0, parts - 1)], num_send).wait_send()
             bytes_of(out_ref.at[pl.ds(0, (parts - 1) * share)], fin_recv).wait_recv()
-        bytes_of(tally, fin_send).wait_send()
+
+    for h in range(sides):
+        @pl.when(serves[h])
+        def _():
+            bytes_of(tally.at[pl.ds(0, n - 1 if h == gate else n)], fin_send).wait_send()
 
 
 def scoped(n, sides, table_width, owners, batch, heads, slots, pairs, *refs):
@@ -489,7 +495,7 @@
     batch, heads, _ = query_rows.shape
     pool = page_table.shape[0]
     rows, pairs = 2 * heads // kv_heads, kv_heads // 2
-    parts = len(owners)
+    parts = len(owners[0])
     share = batch // parts
     f32, bf16 = jnp.float32, jnp.bfloat16
     hbm = pl.BlockSpec(memory_space=pl.ANY)
@@ -515,19 +521,19 @@
             pltpu.VMEM((batch, pairs, rows, page), f32),
             pltpu.VMEM((1, page), jnp.int32),
             pltpu.SMEM((1, page), jnp.int32),
-            pltpu.VMEM((sides, share, heads, head_dim), bf16),
-            pltpu.VMEM((sides * n - 1, share, heads, head_dim), bf16),
+            pltpu.VMEM((share, heads, head_dim), bf16),
+            pltpu.VMEM((n, share, heads, head_dim), bf16),
             pltpu.VMEM((parts, rows, page), f32),
-            pltpu.VMEM((sides * n, rows, page), f32),
+            pltpu.VMEM((n, rows, page), f32),
             pltpu.VMEM((pairs, parts, share * rows, head_dim), f32),
-            pltpu.VMEM((pairs, sides * n, share * rows, head_dim), f32),
+            pltpu.VMEM((pairs, n, share * rows, head_dim), f32),
             dma((3,)),
             dma((KEY_PIECES,)),
             dma((EARLY,)),
             dma,
-            dma((sides,)),
             dma,
-            dma((pairs, sides)),
+            dma,
+            dma((pairs,)),
             dma,
             dma,
         ],
@@ -535,13 +541,14 @@
     )(query_rows, cache_keys, cache_values, page_table, seq_lengths)
 
 
-def owners_of(n):
-    return tuple(range(n // 2 - 2, n // 2 + 2))
+def owners_of(n, sides):
+    even = tuple(range(0, n, n // 4))
+    return tuple(tuple(o + h for o in even) for h in range(sides))
 
 
 def solution(mesh):
     n = mesh.shape["seq"]
-    owners = owners_of(n)
+    owners = owners_of(n, mesh.shape["head"])
     in_specs = (
         P("grp", "head", None),
         P(("grp", "seq"), "head", None, None),

time: 14.3 us -> 14.2 us (level)
  no operation moved by 1% of the time
where the time goes in v4:
time: 14.2 us; the launch traced here: 14 us
  Pallas kernels  13.4 us (94%)
  local copies, waits for them, and re-layouts  0.62 us (4%)
    pallas_call x1, Pallas kernels, shards(): pl.pallas_call(functools.partial(scoped, n, sides, pool // batch, owners,...  13.4 us
    unnamed x1, local copies, waits for them, and re-layouts  0.62 us

profile of v4, /device:TPU:0, one launch (start us, length us, event | category | flops | bytes accessed | tf_op | source)
XLA Modules:
  0.0 14.0 jit_solution(8930279831699000738)
XLA Ops:
  0.0 13.4 %shard_map.55 = bf16[8,16,128]{2,1,0:T(8,128)(2,1)S(1)} custom-call(bf16[8,16,128]{2,1,0:T(8,128)(2,1)} %refs_0_.1, bf16[32,4,128,128]{3,2,1,0:T(8,128)(2,1)} %refs_1_.1, bf16[32,4,128,128]{3,2,1,0:T(8,128)(2,1)} %refs_2_.1, s32[256]{0:T(256)} %refs_3_.1, s32[8]{0:T(128)} %refs_4_.1), custom_call_target="tpu_custom_call" | custom-call | tf_op jit(solution)/shard_map/pallas_call | solution.py:503
  13.4 0.6 %copy.7 = bf16[8,16,128]{2,1,0:T(8,128)(2,1)} copy(bf16[8,16,128]{2,1,0:T(8,128)(2,1)S(1)} %shard_map.55) | data formatting | bytes 65536

commit v5 on v4

--- a/solution.py
+++ b/solution.py
@@ -49,6 +49,11 @@
     row_smem,
     done_ref,
     tally,
+    rest_scale,
+    rest,
+    scale_in,
+    rest_in,
+    far_in,
     stat_out,
     stat_in,
     num_out,
@@ -62,6 +67,12 @@
     num_recv,
     fin_send,
     fin_recv,
+    far_send,
+    far_recv,
+    scale_send,
+    scale_recv,
+    rest_send,
+    rest_recv,
 ):
     me = lax.axis_index("seq")
     side = lax.axis_index("head")
@@ -128,7 +139,15 @@
     targets = [
         sum(jnp.where(side == h, owners[h][i], 0) for h in range(sides)) for i in range(parts)
     ]
+    near, far = 0, n - 1
+    is_near = (side != gate) & (me == near)
+    is_far = (side != gate) & (me == far)
+    late = jnp.where(is_far, 1, 0)
     barrier = pltpu.get_barrier_semaphore()
+
+    @pl.when(is_near)
+    def _():
+        pl.semaphore_signal(barrier, inc=1, device_id={"seq": far}, device_id_type=MESH)
 
     def members(h):
         for seq in range(n - 1 if h == gate else n):
@@ -157,8 +176,18 @@
             src_ref=num_out.at[j, i],
             dst_ref=num_in.at[j, me],
             send_sem=num_send,
-            recv_sem=num_recv.at[j],
+            recv_sem=num_recv.at[j, late],
             device_id={"seq": targets[i], "head": gate},
+            device_id_type=MESH,
+        )
+
+    def near_copy(src, dst, send, recv):
+        return pltpu.make_async_remote_copy(
+            src_ref=src,
+            dst_ref=dst,
+            send_sem=send,
+            recv_sem=recv,
+            device_id={"seq": near, "head": 0},
             device_id_type=MESH,
         )
 
@@ -373,7 +402,7 @@
     def post_stats():
         for i in range(parts):
             stat_out[i] = stats[i]
-        pl.semaphore_wait(barrier, jnp.where(mine, parts - 1, parts))
+        pl.semaphore_wait(barrier, jnp.where(mine, parts - 1, parts) + late)
 
         def keep(i):
             stat_in[me] = stat_out[i]
@@ -386,6 +415,10 @@
 
         def keep(i):
             num_in[j, me] = num_out[j, i]
+
+        @pl.when(is_far)
+        def _():
+            near_copy(num_out.at[j], far_in.at[j], far_send, far_recv).start()
 
         post(lambda i: num_copy(j, i).start(), keep)
 
@@ -422,21 +455,37 @@
         for s in range(n):
             for at in range(pairs * share):
                 columns[s, at] = jnp.broadcast_to(scales[s][:, at : at + 1], (rows, head_dim))
-        blocks = []
+        if h != gate:
+            rest_scale[...] = scales[far]
+            near_copy(rest_scale, scale_in.at[rank], scale_send, scale_recv).start()
+
+        def term(s, j, local):
+            here = pl.ds(local * rows, rows)
+            return columns[s, j * share + local] * num_in[j, s, here, :]
+
+        blocks = {}
         for j in range(pairs):
-            bytes_of(num_in.at[j, pl.ds(0, senders)], num_recv.at[j]).wait_recv()
+            bytes_of(num_in.at[j, pl.ds(0, n - 1)], num_recv.at[j, 0]).wait_recv()
             for local in range(share):
-                here = pl.ds(local * rows, rows)
-                blocks.append(
-                    sum(columns[s, j * share + local] * num_in[j, s, here, :] for s in range(n))
+                blocks[j, local] = sum(
+                    term(s, j, local) for s in range(n) if h == gate or s != far
                 )
+            if h != gate:
+                for local in range(share):
+                    rest[j, pl.ds(local * rows, rows), :] = blocks[j, local]
+                near_copy(rest.at[j], rest_in.at[j, rank], rest_send, rest_recv).start()
+        if h != gate:
+            for j in range(pairs):
+                bytes_of(num_in.at[j, pl.ds(0, 1)], num_recv.at[j, 1]).wait_recv()
+                for local in range(share):
+                    blocks[j, local] = blocks[j, local] + term(far, j, local)
         for local in range(share):
-            whole = [blocks[j * share + local] for j in range(pairs)]
+            whole = [blocks[j, local] for j in range(pairs)]
             whole = jnp.concatenate(whole, axis=0).astype(out_ref.dtype)
             done_ref[local] = whole
             if h == gate:
                 out_ref[rank * share + local] = whole
-        for seq in members(h):
+        for seq in members(h) if h == gate else range(1, n):
             fin_copy(h, seq).start()
 
     for h in range(sides):
@@ -448,7 +497,35 @@
     def _():
         bytes_of(stat_out, stat_send).wait_send()
         bytes_of(num_out, num_send).wait_send()
+
+    @pl.when(is_far)
+    def _():
+        bytes_of(num_out, far_send).wait_send()
+
+    @pl.when(jnp.logical_not(mine | is_near))
+    def _():
         bytes_of(out_ref, fin_recv).wait_recv()
+
+    @pl.when(is_near)
+    def _():
+        bytes_of(scale_in, scale_recv).wait_recv()
+        columns = {}
+        for i in range(parts):
+            for at in range(pairs * share):
+                columns[i, at] = jnp.broadcast_to(
+                    scale_in[i][:, at : at + 1], (rows, head_dim)
+                )
+        bytes_of(rest_in, rest_recv).wait_recv()
+        bytes_of(far_in, far_recv).wait_recv()
+        for i in range(parts):
+            for local in range(share):
+                here = pl.ds(local * rows, rows)
+                whole = [
+                    rest_in[j, i, here, :] + columns[i, j * share + local] * far_in[j, i, here, :]
+                    for j in range(pairs)
+                ]
+                whole = jnp.concatenate(whole, axis=0).astype(out_ref.dtype)
+                out_ref[i * share + local] = whole
 
     @pl.when(mine)
     def _():
@@ -460,7 +537,10 @@
     for h in range(sides):
         @pl.when(serves[h])
         def _():
-            bytes_of(tally.at[pl.ds(0, n - 1 if h == gate else n)], fin_send).wait_send()
+            bytes_of(tally, fin_send).wait_send()
+            if h != gate:
+                bytes_of(rest_scale, scale_send).wait_send()
+                bytes_of(rest, rest_send).wait_send()
 
 
 def scoped(n, sides, table_width, owners, batch, heads, slots, pairs, *refs):
@@ -522,7 +602,12 @@
             pltpu.VMEM((1, page), jnp.int32),
             pltpu.SMEM((1, page), jnp.int32),
             pltpu.VMEM((share, heads, head_dim), bf16),
-            pltpu.VMEM((n, share, heads, head_dim), bf16),
+            pltpu.VMEM((n - 1, share, heads, head_dim), bf16),
+            pltpu.VMEM((rows, page), f32),
+            pltpu.VMEM((pairs, share * rows, head_dim), f32),
+            pltpu.VMEM((parts, rows, page), f32),
+            pltpu.VMEM((pairs, parts, share * rows, head_dim), f32),
+            pltpu.VMEM((pairs, parts, share * rows, head_dim), f32),
             pltpu.VMEM((parts, rows, page), f32),
             pltpu.VMEM((n, rows, page), f32),
             pltpu.VMEM((pairs, parts, share * rows, head_dim), f32),
@@ -533,7 +618,13 @@
             dma,
             dma,
             dma,
-            dma((pairs,)),
+            dma((pairs, 2)),
+            dma,
+            dma,
+            dma,
+            dma,
+            dma,
+            dma,
             dma,
             dma,
         ],

time: 14.2 us -> 14 us (0.986)
  Pallas kernels: 13.4 us -> 13.2 us
    pallas_call x1, Pallas kernels: 13.4 us -> 13.2 us  [shards(): pl.pallas_call(functools.partial(scoped, n, sides, pool // batch, owners,...]
where the time goes in v5:
time: 14 us; the launch traced here: 13.9 us
  Pallas kernels  13.2 us (94%)
  local copies, waits for them, and re-layouts  0.62 us (4%)
    pallas_call x1, Pallas kernels, shards(): pl.pallas_call(functools.partial(scoped, n, sides, pool // batch, owners,...  13.2 us
    unnamed x1, local copies, waits for them, and re-layouts  0.62 us

profile of v5, /device:TPU:0, one launch (start us, length us, event | category | flops | bytes accessed | tf_op | source)
XLA Modules:
  0.0 13.9 jit_solution(2732629225559521807)
XLA Ops:
  0.0 13.2 %shard_map.55 = bf16[8,16,128]{2,1,0:T(8,128)(2,1)S(1)} custom-call(bf16[8,16,128]{2,1,0:T(8,128)(2,1)} %refs_0_.1, bf16[32,4,128,128]{3,2,1,0:T(8,128)(2,1)} %refs_1_.1, bf16[32,4,128,128]{3,2,1,0:T(8,128)(2,1)} %refs_2_.1, s32[256]{0:T(256)} %refs_3_.1, s32[8]{0:T(128)} %refs_4_.1), custom_call_target="tpu_custom_call" | custom-call | tf_op jit(solution)/shard_map/pallas_call | solution.py:583
  13.2 0.6 %copy.7 = bf16[8,16,128]{2,1,0:T(8,128)(2,1)} copy(bf16[8,16,128]{2,1,0:T(8,128)(2,1)S(1)} %shard_map.55) | data formatting | bytes 65536

commit v6 on v5

--- a/solution.py
+++ b/solution.py
@@ -13,9 +13,8 @@
 FLOOR = -1e29
 KEY_PIECES = 8
 VALUE_PIECES = ((1, 1, 1, 1), (2, 2, 2, 1, 1))
-EARLY = 1
-STEP = 1
-PAUSE = 40
+WINDOW = 8
+PAUSE = 20
 
 
 def attend(
@@ -60,7 +59,6 @@
     num_in,
     small_sem,
     k_sem,
-    v_sem,
     stat_send,
     stat_recv,
     num_send,
@@ -93,41 +91,6 @@
     )
     for copy in small:
         copy.start()
-    pl.delay(PAUSE)
-    span = slots // KEY_PIECES
-    k_copies = [
-        pltpu.make_async_copy(
-            k_hbm.at[pl.ds(i * span, span)], k_vmem.at[pl.ds(i * span, span)], k_sem.at[i]
-        )
-        for i in range(KEY_PIECES)
-    ]
-    v_copies = []
-    for j in range(pairs):
-        cuts = VALUE_PIECES[min(j, 1)]
-        unit, at = slots // sum(cuts), 0
-        for size in cuts:
-            pages = pl.ds(at, size * unit)
-            v_copies.append(
-                (
-                    j,
-                    at,
-                    size * unit,
-                    pltpu.make_async_copy(
-                        v_hbm.at[pages, pl.ds(2 * j, 2)],
-                        v_vmem.at[pages, pl.ds(2 * j, 2)],
-                        v_sem.at[len(v_copies)]
-                        if len(v_copies) < EARLY
-                        else k_sem.at[len(v_copies) - EARLY],
-                    ),
-                )
-            )
-            at += size * unit
-    for copy in k_copies:
-        copy.start()
-    unstarted = [copy for _, _, _, copy in v_copies]
-    for _ in range(EARLY):
-        unstarted.pop(0).start()
-
     serves = [
         (side == gate) & functools.reduce(lambda a, b: a | b, [me == o for o in owners[h]])
         for h in range(sides)
@@ -145,10 +108,6 @@
     late = jnp.where(is_far, 1, 0)
     barrier = pltpu.get_barrier_semaphore()
 
-    @pl.when(is_near)
-    def _():
-        pl.semaphore_signal(barrier, inc=1, device_id={"seq": far}, device_id_type=MESH)
-
     def members(h):
         for seq in range(n - 1 if h == gate else n):
             yield jnp.where(me <= seq, seq + 1, seq) if h == gate else seq
@@ -160,6 +119,49 @@
                 pl.semaphore_signal(
                     barrier, inc=1, device_id={"seq": seq, "head": h}, device_id_type=MESH
                 )
+
+    @pl.when(is_near)
+    def _():
+        pl.semaphore_signal(barrier, inc=1, device_id={"seq": far}, device_id_type=MESH)
+
+    pl.delay(PAUSE)
+    span = slots // KEY_PIECES
+    k_copies = [
+        pltpu.make_async_copy(
+            k_hbm.at[pl.ds(i * span, span)], k_vmem.at[pl.ds(i * span, span)], k_sem.at[i]
+        )
+        for i in range(KEY_PIECES)
+    ]
+    v_copies = []
+
+    def source(item):
+        return item if item < KEY_PIECES else source(item - WINDOW)
+
+    for j in range(pairs):
+        cuts = VALUE_PIECES[min(j, 1)]
+        unit, at = slots // sum(cuts), 0
+        for size in cuts:
+            pages = pl.ds(at, size * unit)
+            v_copies.append(
+                (
+                    j,
+                    at,
+                    size * unit,
+                    pltpu.make_async_copy(
+                        v_hbm.at[pages, pl.ds(2 * j, 2)],
+                        v_vmem.at[pages, pl.ds(2 * j, 2)],
+                        k_sem.at[source(KEY_PIECES + len(v_copies))],
+                    ),
+                )
+            )
+            at += size * unit
+    unstarted = k_copies + [copy for _, _, _, copy in v_copies]
+
+    def begin(count):
+        for _ in range(min(count, len(unstarted))):
+            unstarted.pop(0).start()
+
+    begin(WINDOW)
 
     def stat_copy(i):
         return pltpu.make_async_remote_copy(
@@ -315,8 +317,7 @@
     for i in range(KEY_PIECES + 1):
         if i < KEY_PIECES:
             k_copies[i].wait()
-            for _ in range(min(STEP, len(unstarted))):
-                unstarted.pop(0).start()
+            begin(1)
             for pp in range(i * span // 2, (i + 1) * span // 2):
                 for j in range(pairs):
                     score(pp, j)
@@ -331,8 +332,6 @@
                         settle(2 * pp + k, j, found)
 
     row_copy.wait()
-    for copy in unstarted:
-        copy.start()
     for key in peaks:
         j, b = key
         peaks[key] = jnp.maximum(jnp.max(peaks[key], axis=1, keepdims=True), FLOOR)
@@ -428,6 +427,7 @@
     owed = None
     for j, at, size, copy in v_copies:
         copy.wait()
+        begin(1)
         gather(j, at, size)
         if j == 0:
             for p in range(at + size, min(at + size + first, slots)):
@@ -614,7 +614,6 @@
             pltpu.VMEM((pairs, n, share * rows, head_dim), f32),
             dma((3,)),
             dma((KEY_PIECES,)),
-            dma((EARLY,)),
             dma,
             dma,
             dma,

time: 14 us -> 14 us (level)
  no operation moved by 1% of the time
where the time goes in v6:
time: 14 us; the launch traced here: 13.9 us
  Pallas kernels  13.2 us (94%)
  local copies, waits for them, and re-layouts  0.62 us (4%)
    pallas_call x1, Pallas kernels, shards(): pl.pallas_call(functools.partial(scoped, n, sides, pool // batch, owners,...  13.2 us
    unnamed x1, local copies, waits for them, and re-layouts  0.62 us

profile of v6, /device:TPU:0, one launch (start us, length us, event | category | flops | bytes accessed | tf_op | source)
XLA Modules:
  0.0 13.9 jit_solution(2894378437401022670)
XLA Ops:
  0.0 13.2 %shard_map.55 = bf16[8,16,128]{2,1,0:T(8,128)(2,1)S(1)} custom-call(bf16[8,16,128]{2,1,0:T(8,128)(2,1)} %refs_0_.1, bf16[32,4,128,128]{3,2,1,0:T(8,128)(2,1)} %refs_1_.1, bf16[32,4,128,128]{3,2,1,0:T(8,128)(2,1)} %refs_2_.1, s32[256]{0:T(256)} %refs_3_.1, s32[8]{0:T(128)} %refs_4_.1), custom_call_target="tpu_custom_call" | custom-call | tf_op jit(solution)/shard_map/pallas_call | solution.py:583
  13.2 0.6 %copy.7 = bf16[8,16,128]{2,1,0:T(8,128)(2,1)} copy(bf16[8,16,128]{2,1,0:T(8,128)(2,1)S(1)} %shard_map.55) | data formatting | bytes 65536
